TPU v7x, 32 devices: a whole 2x2x4 slice. The times are simulated.
32 devices in a mesh: row: 8 (over y, x, core), col: 4 (over z).
Axes of the slice: x: 2, y: 2, z: 4, core: 2. Of those that a mesh axis runs over, the one named last changes fastest.
Arguments:
- trailing: bfloat16 [4096, 8192], P('row', 'col'), may hold values from -6 to 6
- col_u: bfloat16 [8, 512, 64], P('row', 'col'), may hold values from -6 to 6
- col_v: bfloat16 [8, 512, 64], P('row', 'col'), may hold values from -0.75 to 0.75
- row_u: bfloat16 [16, 512, 64], P('col', 'row'), may hold values from -6 to 6
- row_v: bfloat16 [16, 512, 64], P('col', 'row'), may hold values from -0.03125 to 0.03125
- diag_lower_inv: float32 [512, 512], replicated, may hold values from -0.176776695 to 1, as said below
- diag_upper_inv: float32 [512, 512], replicated, may hold values from -0.176776695 to 2, as said below
Outputs:
- schur: bfloat16 [4096, 8192], P('row', 'col')
Inputs may be any that keep to these rules, and one draw needn't show every extreme that they name: `diag_lower_inv`: lower triangular with unit diagonal. `diag_upper_inv`: upper triangular with diagonal entries between 0.5 and 2.
All inputs are finite; a program needn't handle non-finite values.
Results may differ from a plain program's by a relative error of at most 0.0054.
Values may be sent and summed in bfloat16 or wider, within the bound.
A program may use at most 64 MiB of HBM per device.

v0:
```python
import functools

import jax
import jax.numpy as jnp
from jax import lax
from jax.experimental import pallas as pl
from jax.experimental.pallas import tpu as pltpu
from jax.sharding import PartitionSpec as P

MESH = pl.DeviceIdType.MESH
F32 = jnp.float32
BF16 = jnp.bfloat16
BLOCKS = 1


def partner(at, step, count):
    if count & (count - 1):
        return lax.rem(at + step, count)
    out = jnp.int32(0)
    weight = 1
    while weight < count:
        bit = (at // weight) % 2
        out = out + weight * ((1 - bit) if step & weight else bit)
        weight *= 2
    return out


def source(at, step, count):
    if count & (count - 1):
        return lax.rem(at + count - step, count)
    return partner(at, step, count)


def split(x):
    high = x.astype(BF16)
    return high, (x - high.astype(F32)).astype(BF16)


def dot(a, b):
    return lax.dot_general(a, b, (((1,), (0,)), ((), ())), preferred_element_type=F32)


def dot_rt(a, b):
    return lax.dot_general(a, b, (((1,), (1,)), ((), ())), preferred_element_type=F32)


def pack(left, right):
    return jnp.concatenate([left.astype(F32), right.astype(F32)], axis=-1).astype(BF16)


def panel_kernel(
    n_row, n_col,
    cu_hbm, cv_hbm, ru_hbm, rv_hbm, dl_hbm, du_hbm, trail_hbm,
    t_ref, cu_ref, trail,
    ru, rv, dl, du, mh, ml, cuall, cvall, gall,
    in_sem, cu_send, cu_recv, cv_send, cv_recv, row_send, row_recv, fwd_send,
):
    row = lax.axis_index("row")
    col = lax.axis_index("col")
    paired = n_row % 2 == 0
    width = 2 if paired else 1
    chips = n_row // width
    core = row % width
    chip = row // width

    col_steps = list(range(n_col - 1, 0, -1))
    chip_steps = list(range(chips - 1, 0, -1))
    col_to = {k: partner(col, k, n_col) for k in col_steps}
    col_from = {k: source(col, k, n_col) for k in col_steps}
    row_to = {k: partner(chip, k, chips) * width + core for k in chip_steps}
    row_from = {k: source(chip, k, chips) * width + core for k in chip_steps}
    mate = chip * width + (1 - core) if paired else row

    barrier = pltpu.get_barrier_semaphore()
    peers = [(row, col_to[k]) for k in col_steps] + [(row_to[k], col) for k in chip_steps]
    if paired:
        peers.append((mate, col))
    for peer in peers:
        pl.semaphore_signal(barrier, inc=1, device_id=peer, device_id_type=MESH)

    loads = []
    for n, (src, dst) in enumerate([
        (ru_hbm, ru), (rv_hbm, rv), (cv_hbm, cvall.at[col]), (cu_hbm, cuall.at[col]),
        (dl_hbm, dl), (du_hbm, du), (trail_hbm, trail),
    ]):
        load = pltpu.make_async_copy(src, dst, in_sem.at[n])
        load.start()
        loads.append(load)

    loads[0].wait()
    loads[1].wait()
    gall[row] = pack(ru[...], rv[...])
    loads[2].wait()
    loads[3].wait()

    pl.semaphore_wait(barrier, len(peers))

    def row_copy(slot, send_sem, to):
        return pltpu.make_async_remote_copy(
            src_ref=gall.at[slot], dst_ref=gall.at[slot], send_sem=send_sem,
            recv_sem=row_recv.at[slot], device_id=(to, col), device_id_type=MESH,
        )

    def col_copy(slots, recv, slot, send_sem, to):
        return pltpu.make_async_remote_copy(
            src_ref=slots.at[slot], dst_ref=slots.at[slot], send_sem=send_sem,
            recv_sem=recv.at[slot], device_id=(row, to), device_id_type=MESH,
        )

    sends = []
    for k in chip_steps:
        sends.append(row_copy(row, row_send.at[k], row_to[k]))
        sends[-1].start()
    for k in col_steps:
        sends.append(col_copy(cvall, cv_recv, col, cv_send.at[k], col_to[k]))
        sends[-1].start()
    for k in col_steps:
        sends.append(col_copy(cuall, cu_recv, col, cu_send.at[k], col_to[k]))
        sends[-1].start()
    if paired:
        sends.append(row_copy(row, row_send.at[0], mate))
        sends[-1].start()

    loads[4].wait()
    loads[5].wait()
    order = dl.shape[0]
    half = order // 2
    uh, ul = split(du[...])
    lh, ll = split(dl[...])

    def product(rows, mid, cols):
        a, b = uh[rows, mid], ul[rows, mid]
        c, d = lh[mid, cols], ll[mid, cols]
        return dot(a, c) + (dot(a, d) + dot(b, c))

    lo, hi, full = slice(0, half), slice(half, order), slice(0, order)
    for rows, mid, cols in ((lo, full, lo), (lo, hi, hi), (hi, hi, lo), (hi, hi, hi)):
        mh[rows, cols], ml[rows, cols] = split(product(rows, mid, cols))

    for k in reversed(chip_steps):
        slot = row_from[k]
        row_copy(slot, row_send.at[k], row_to[k]).wait_recv()
        if paired:
            sends.append(row_copy(slot, fwd_send.at[k], mate))
            sends[-1].start()

    tiles, rank = cvall.shape[1], cvall.shape[2]
    for k in reversed(col_steps):
        col_copy(cvall, cv_recv, col_from[k], cv_send.at[k], col_to[k]).wait_recv()
    weights = []
    for t in range(tiles):
        turned = jnp.concatenate([cvall[c, t] for c in range(n_col)], axis=-1)
        wh, wl = split(dot(turned, mh[...]) + dot(turned, ml[...]))
        weights.append(jnp.concatenate([wh, wl], axis=0))

    for k in reversed(col_steps):
        col_copy(cuall, cu_recv, col_from[k], cu_send.at[k], col_to[k]).wait_recv()
    lefts = []
    for t in range(tiles):
        turned = jnp.concatenate([cuall[c, t] for c in range(n_col)], axis=-1).astype(F32)
        lefts.append(jnp.concatenate([turned, turned], axis=0).T.astype(BF16))

    if paired:
        row_copy(mate, row_send.at[0], mate).wait_recv()
        for k in reversed(chip_steps):
            slot = source(chip, k, chips) * width + (1 - core)
            row_copy(slot, fwd_send.at[k], mate).wait_recv()
    loads[6].wait()

    panels = [gall[:, j].reshape(order, 2 * rank) for j in range(gall.shape[1])]
    spread = jnp.concatenate(panels, axis=-1)
    for t in range(tiles):
        c = dot(weights[t], spread)
        c = c[:rank] + c[rank:]
        rights = []
        for j, g in enumerate(panels):
            core_j = c[:, 2 * rank * j:2 * rank * j + rank]
            ch, cl = split(jnp.concatenate([jnp.zeros_like(core_j), core_j], axis=-1))
            right = dot_rt(jnp.concatenate([ch, cl], axis=0), g)
            th, tl = split(right[:rank] + right[rank:])
            rights.append(jnp.concatenate([th, tl], axis=0))
        cu_ref[t] = lefts[t]
        for j, right in enumerate(rights):
            t_ref[t, :, pl.ds(j * order, order)] = right

    for send in sends:
        send.wait_send()


def update_kernel(blocks, t_ref, cu_ref, trail, out_hbm, out, out_sem):
    tiles, order, _ = cu_ref.shape
    wide = t_ref.shape[2] // blocks
    copies = []
    for t in range(tiles):
        rows = pl.ds(t * order, order)
        for b in range(blocks):
            at = pl.ds(b * wide, wide)
            product = dot(cu_ref[t], t_ref[t, :, at])
            out[rows, at] = (trail[rows, at].astype(F32) - product).astype(BF16)
            copy = pltpu.make_async_copy(out.at[rows, at], out_hbm.at[rows, at], out_sem.at[t * blocks + b])
            copy.start()
            copies.append(copy)
    for copy in copies:
        copy.wait()


def shards(n_row, n_col, trailing, col_u, col_v, row_u, row_v, diag_lower_inv, diag_upper_inv):
    mt, cc, rank = col_u.shape
    nt, rc, _ = row_u.shape
    order = diag_lower_inv.shape[0]
    anywhere = pl.BlockSpec(memory_space=pl.ANY)
    dma = pltpu.SemaphoreType.DMA
    wide = nt * order
    vmem = pl.BlockSpec(memory_space=pltpu.VMEM)
    handed = pl.pallas_call(
        functools.partial(panel_kernel, n_row, n_col),
        out_shape=[
            pltpu.VMEM((mt, 2 * rank, wide), BF16),
            pltpu.VMEM((mt, order, 2 * rank), BF16),
            pltpu.VMEM(trailing.shape, BF16),
        ],
        in_specs=[anywhere] * 7,
        out_specs=[vmem] * 3,
        scratch_shapes=[
            pltpu.VMEM(row_u.shape, BF16),
            pltpu.VMEM(row_v.shape, BF16),
            pltpu.VMEM((order, order), F32),
            pltpu.VMEM((order, order), F32),
            pltpu.VMEM((order, order), BF16),
            pltpu.VMEM((order, order), BF16),
            pltpu.VMEM((n_col, mt, rank, cc), BF16),
            pltpu.VMEM((n_col, mt, rank, cc), BF16),
            pltpu.VMEM((n_row, nt, rc, 2 * rank), BF16),
            dma((7,)), dma((n_col,)), dma((n_col,)), dma((n_col,)), dma((n_col,)),
            dma((n_row,)), dma((n_row,)), dma((n_row,)),
        ],
        compiler_params=pltpu.CompilerParams(collective_id=0, has_side_effects=True),
        name="panels",
    )(
        jnp.swapaxes(col_u, 1, 2), jnp.swapaxes(col_v, 1, 2), row_u, row_v,
        diag_lower_inv, diag_upper_inv, trailing,
    )
    handed = [pltpu.with_memory_space_constraint(x, pltpu.VMEM) for x in handed]
    blocks = BLOCKS * nt
    return pl.pallas_call(
        functools.partial(update_kernel, blocks),
        out_shape=jax.ShapeDtypeStruct(trailing.shape, BF16),
        in_specs=[vmem] * 3,
        out_specs=anywhere,
        scratch_shapes=[pltpu.VMEM(trailing.shape, BF16), dma((mt * blocks,))],
        name="update",
    )(*handed)


def solution(mesh):
    placed = (
        P("row", "col"),
        P("row", "col", None),
        P("row", "col", None),
        P("col", "row", None),
        P("col", "row", None),
        P(),
        P(),
    )
    return jax.shard_map(
        functools.partial(shards, mesh.shape["row"], mesh.shape["col"]),
        mesh=mesh, in_specs=placed, out_specs=P("row", "col"), check_vma=False,
    )
```

profile of v0, /device:TPU:1, one launch (start us, length us, event | category | flops | bytes accessed | tf_op | source)
XLA Modules:
  0.0 13.5 jit_solution(7967120743054139172)
XLA Ops:
  0.0 11.8 %panels.1 = (bf16[1,128,2048]{2,1,0:T(8,128)(2,1)S(1)}, bf16[1,512,128]{2,1,0:T(8,128)(2,1)S(1)}, bf16[512,2048]{1,0:T(8,128)(2,1)S(1)}) custom-call(bf16[1,64,128]{2,1,0:T(8,128)(2,1)} %bitcast.2, bf16[1,64,128]{2,1,0:T(8,128)(2,1)} %bitcast.3, bf16[4,64,64]{2,1,0:T(8,128)(2,1)} %ru_hbm.1, bf16[4,64,64]{2,1,0:T(8,128)(2,1)} %rv_hbm.1, f32[512,512]{1,0:T(8,128)} %dl_hbm.1, ...), custom_call_target="tpu_custom_call" | custom-call | tf_op jit(solution)/shard_map/panels/pallas_call | solution.py:215
  11.8 1.6 %update.1 = bf16[512,2048]{1,0:T(8,128)(2,1)} custom-call(bf16[1,128,2048]{2,1,0:T(8,128)(2,1)S(1)} %get-tuple-element.8.t_ref, bf16[1,512,128]{2,1,0:T(8,128)(2,1)S(1)} %get-tuple-element.9.cu_ref, bf16[512,2048]{1,0:T(8,128)(2,1)S(1)} %get-tuple-element.10.trail), custom_call_target="tpu_custom_call" | custom-call | tf_op jit(solution)/shard_map/update/pallas_call | solution.py:245
where the time goes:
time: 13.6 us; the launch traced here: 13.5 us
  Pallas kernels  13.4 us (99%)
    pallas_call x1, Pallas kernels, shards(): pl.pallas_call(functools.partial(panel_kernel, n_row, n_col), out_shape=[...  11.8 us
    pallas_call x1, Pallas kernels, shards(): pl.pallas_call(functools.partial(update_kernel, blocks), out_shape=jax.Sh...  1.63 us

commit v1 on v0

--- a/solution.py
+++ b/solution.py
@@ -53,7 +53,7 @@
     cu_hbm, cv_hbm, ru_hbm, rv_hbm, dl_hbm, du_hbm, trail_hbm,
     t_ref, cu_ref, trail,
     ru, rv, dl, du, mh, ml, cuall, cvall, gall,
-    in_sem, cu_send, cu_recv, cv_send, cv_recv, row_send, row_recv, fwd_send,
+    in_sem, cu_send, cu_recv, cv_send, cv_recv, row_send, row_recv, fwd_send, row_hello, col_hello,
 ):
     row = lax.axis_index("row")
     col = lax.axis_index("col")
@@ -71,12 +71,20 @@
     row_from = {k: source(chip, k, chips) * width + core for k in chip_steps}
     mate = chip * width + (1 - core) if paired else row
 
+    col_peers = [col_to[k] for k in col_steps]
+    chip_peers = [row_to[k] for k in chip_steps]
+    if paired:
+        chip_peers.append(mate)
+
     barrier = pltpu.get_barrier_semaphore()
-    peers = [(row, col_to[k]) for k in col_steps] + [(row_to[k], col) for k in chip_steps]
-    if paired:
-        peers.append((mate, col))
-    for peer in peers:
-        pl.semaphore_signal(barrier, inc=1, device_id=peer, device_id_type=MESH)
+    for to in chip_peers:
+        @pl.when(to > row)
+        def _():
+            pl.semaphore_signal(barrier, inc=1, device_id=(to, col), device_id_type=MESH)
+    for to in col_peers:
+        @pl.when(to > col)
+        def _():
+            pl.semaphore_signal(barrier, inc=1, device_id=(row, to), device_id_type=MESH)
 
     loads = []
     for n, (src, dst) in enumerate([
@@ -87,14 +95,27 @@
         load.start()
         loads.append(load)
 
+    lower = chip + (core if paired else 0) + col
+
+    @pl.when(lower > 0)
+    def _():
+        pl.semaphore_wait(barrier, lower)
+
+    for to in chip_peers:
+        @pl.when(to < row)
+        def _():
+            pl.semaphore_signal(row_hello.at[row], inc=1, device_id=(to, col), device_id_type=MESH)
+    for to in col_peers:
+        @pl.when(to < col)
+        def _():
+            pl.semaphore_signal(col_hello.at[col], inc=1, device_id=(row, to), device_id_type=MESH)
+
     loads[0].wait()
     loads[1].wait()
     gall[row] = pack(ru[...], rv[...])
     loads[2].wait()
     loads[3].wait()
 
-    pl.semaphore_wait(barrier, len(peers))
-
     def row_copy(slot, send_sem, to):
         return pltpu.make_async_remote_copy(
             src_ref=gall.at[slot], dst_ref=gall.at[slot], send_sem=send_sem,
@@ -107,19 +128,19 @@
             recv_sem=recv.at[slot], device_id=(row, to), device_id_type=MESH,
         )
 
-    sends = []
-    for k in chip_steps:
-        sends.append(row_copy(row, row_send.at[k], row_to[k]))
-        sends[-1].start()
-    for k in col_steps:
-        sends.append(col_copy(cvall, cv_recv, col, cv_send.at[k], col_to[k]))
-        sends[-1].start()
-    for k in col_steps:
-        sends.append(col_copy(cuall, cu_recv, col, cu_send.at[k], col_to[k]))
-        sends[-1].start()
+    row_sends = [(row_to[k], row_copy(row, row_send.at[k], row_to[k])) for k in chip_steps]
     if paired:
-        sends.append(row_copy(row, row_send.at[0], mate))
-        sends[-1].start()
+        row_sends.append((mate, row_copy(row, row_send.at[0], mate)))
+    col_sends = [
+        (col_to[k], col_copy(slots, recv, col, send.at[k], col_to[k]))
+        for slots, recv, send in ((cvall, cv_recv, cv_send), (cuall, cu_recv, cu_send))
+        for k in col_steps
+    ]
+    for to, copy in col_sends:
+        pl.when(to < col)(copy.start)
+    for to, copy in row_sends:
+        pl.when(to < row)(copy.start)
+    sends = [copy for _, copy in row_sends + col_sends]
 
     loads[4].wait()
     loads[5].wait()
@@ -136,6 +157,20 @@
     lo, hi, full = slice(0, half), slice(half, order), slice(0, order)
     for rows, mid, cols in ((lo, full, lo), (lo, hi, hi), (hi, hi, lo), (hi, hi, hi)):
         mh[rows, cols], ml[rows, cols] = split(product(rows, mid, cols))
+
+    for to, copy in reversed(row_sends):
+        @pl.when(to > row)
+        def _():
+            pl.semaphore_wait(row_hello.at[to], 1)
+            copy.start()
+    for k in reversed(col_steps):
+        to = col_to[k]
+
+        @pl.when(to > col)
+        def _():
+            pl.semaphore_wait(col_hello.at[to], 1)
+            col_copy(cvall, cv_recv, col, cv_send.at[k], to).start()
+            col_copy(cuall, cu_recv, col, cu_send.at[k], to).start()
 
     for k in reversed(chip_steps):
         slot = row_from[k]
@@ -233,6 +268,7 @@
             pltpu.VMEM((n_row, nt, rc, 2 * rank), BF16),
             dma((7,)), dma((n_col,)), dma((n_col,)), dma((n_col,)), dma((n_col,)),
             dma((n_row,)), dma((n_row,)), dma((n_row,)),
+            pltpu.SemaphoreType.REGULAR((n_row,)), pltpu.SemaphoreType.REGULAR((n_col,)),
         ],
         compiler_params=pltpu.CompilerParams(collective_id=0, has_side_effects=True),
         name="panels",

time: 13.6 us -> 11.7 us (0.86)
  the two profiles are of different devices: /device:TPU:1 before, /device:TPU:0 now
where the time goes in v1:
time: 11.7 us; the launch traced here: 11.6 us
  Pallas kernels  11.6 us (99%)
    pallas_call x1, Pallas kernels, shards(): pl.pallas_call(functools.partial(panel_kernel, n_row, n_col), out_shape=[...  9.92 us
    pallas_call x1, Pallas kernels, shards(): pl.pallas_call(functools.partial(update_kernel, blocks), out_shape=jax.Sh...  1.63 us

profile of v1, /device:TPU:0, one launch (start us, length us, event | category | flops | bytes accessed | tf_op | source)
XLA Modules:
  0.0 11.6 jit_solution(9937220005633537956)
XLA Ops:
  0.0 9.9 %panels.1 = (bf16[1,128,2048]{2,1,0:T(8,128)(2,1)S(1)}, bf16[1,512,128]{2,1,0:T(8,128)(2,1)S(1)}, bf16[512,2048]{1,0:T(8,128)(2,1)S(1)}) custom-call(bf16[1,64,128]{2,1,0:T(8,128)(2,1)} %bitcast.2, bf16[1,64,128]{2,1,0:T(8,128)(2,1)} %bitcast.3, bf16[4,64,64]{2,1,0:T(8,128)(2,1)} %ru_hbm.1, bf16[4,64,64]{2,1,0:T(8,128)(2,1)} %rv_hbm.1, f32[512,512]{1,0:T(8,128)} %dl_hbm.1, ...), custom_call_target="tpu_custom_call" | custom-call | tf_op jit(solution)/shard_map/panels/pallas_call | solution.py:250
  9.9 1.6 %update.1 = bf16[512,2048]{1,0:T(8,128)(2,1)} custom-call(bf16[1,128,2048]{2,1,0:T(8,128)(2,1)S(1)} %get-tuple-element.8.t_ref, bf16[1,512,128]{2,1,0:T(8,128)(2,1)S(1)} %get-tuple-element.9.cu_ref, bf16[512,2048]{1,0:T(8,128)(2,1)S(1)} %get-tuple-element.10.trail), custom_call_target="tpu_custom_call" | custom-call | tf_op jit(solution)/shard_map/update/pallas_call | solution.py:281

commit v2 on v0

v2 whole, which is shorter than its diff:
```python
import functools

import jax
import jax.numpy as jnp
from jax import lax
from jax.experimental import pallas as pl
from jax.experimental.pallas import tpu as pltpu
from jax.sharding import PartitionSpec as P

MESH = pl.DeviceIdType.MESH
F32 = jnp.float32
BF16 = jnp.bfloat16
LANES = 128
BLOCKS = 1


def others(at, count):
    if count & (count - 1):
        return [(step, lax.rem(at + step, count), count - step) for step in range(1, count)]
    out = []
    for step in range(1, count):
        to, weight = jnp.int32(0), 1
        while weight < count:
            bit = (at // weight) % 2
            to = to + weight * ((1 - bit) if step & weight else bit)
            weight *= 2
        out.append((step, to, step))
    return out


def split(x):
    high = x.astype(BF16)
    return high, (x - high.astype(F32)).astype(BF16)


def dot(a, b):
    return lax.dot_general(a, b, (((1,), (0,)), ((), ())), preferred_element_type=F32)


def dot_rt(a, b):
    return lax.dot_general(a, b, (((1,), (1,)), ((), ())), preferred_element_type=F32)


def pack(x, width):
    if width == 1:
        return x
    x = x.astype(F32)
    return jnp.stack([
        jnp.concatenate([x[p * width + w] for w in range(width)], axis=-1)
        for p in range(x.shape[0] // width)
    ]).astype(BF16)


def panel_kernel(
    n_row, n_col, order, rank,
    cu_hbm, cv_hbm, ru_hbm, rv_hbm, dl_hbm, du_hbm, trail_hbm,
    d_ref, gvall, trail,
    ru, rv, dl, du, mh, ml, cuall, cvall, guall,
    in_sem, cu_send, cu_recv, cv_send, cv_recv, gu_send, gu_recv, gv_send, gv_recv,
    row_hello, col_hello,
):
    row = lax.axis_index("row")
    col = lax.axis_index("col")
    paired = n_row % 2 == 0
    width = 2 if paired else 1
    chips = n_row // width
    core = row % width
    chip = row // width
    mate = chip * width + (1 - core) if paired else row
    nt, pieces = ru.shape[0], guall.shape[1]
    wide = nt // pieces

    near = [(step, to * width + core, back) for step, to, back in others(chip, chips)]
    near_cols = others(col, n_col)
    row_peers = ([(0, mate, 0)] if paired else []) + near

    barrier = pltpu.get_barrier_semaphore()
    for _, to, _ in row_peers:
        @pl.when(to > row)
        def _():
            pl.semaphore_signal(barrier, inc=1, device_id=(to, col), device_id_type=MESH)
    for _, to, _ in near_cols:
        @pl.when(to > col)
        def _():
            pl.semaphore_signal(barrier, inc=1, device_id=(row, to), device_id_type=MESH)

    loads = []
    for n, (src, dst) in enumerate([
        (ru_hbm, ru), (rv_hbm, rv), (cv_hbm, cvall.at[col]), (cu_hbm, cuall.at[col]),
        (dl_hbm, dl), (du_hbm, du), (trail_hbm, trail),
    ]):
        load = pltpu.make_async_copy(src, dst, in_sem.at[n])
        load.start()
        loads.append(load)

    lower_row = chip + (core if paired else 0)
    lower_col = col
    higher_row = len(row_peers) - lower_row
    higher_col = len(near_cols) - lower_col

    @pl.when(lower_row + lower_col > 0)
    def _():
        pl.semaphore_wait(barrier, lower_row + lower_col)

    for _, to, _ in row_peers:
        @pl.when(to < row)
        def _():
            pl.semaphore_signal(row_hello, inc=1, device_id=(to, col), device_id_type=MESH)
    for _, to, _ in near_cols:
        @pl.when(to < col)
        def _():
            pl.semaphore_signal(col_hello, inc=1, device_id=(row, to), device_id_type=MESH)

    def row_copy(buf, slot, send, recv, to):
        return pltpu.make_async_remote_copy(
            src_ref=buf.at[slot], dst_ref=buf.at[slot], send_sem=send, recv_sem=recv,
            device_id=(to, col), device_id_type=MESH,
        )

    def col_send(src, buf, send, recv, to):
        return pltpu.make_async_remote_copy(
            src_ref=src, dst_ref=buf.at[col], send_sem=send, recv_sem=recv,
            device_id=(row, to), device_id_type=MESH,
        )

    def cols_to(to):
        col_send(cv_hbm, cvall, cv_send, cv_recv, to).start()
        col_send(cu_hbm, cuall, cu_send, cu_recv, to).start()

    def rows_to(to, back):
        row_copy(guall, row, gu_send, gu_recv.at[back], to).start()
        row_copy(gvall, row, gv_send, gv_recv.at[back], to).start()

    for to in range(n_col):
        @pl.when(to < col)
        def _():
            cols_to(to)
    loads[0].wait()
    loads[1].wait()
    guall[row] = pack(ru[...], wide)
    gvall[row] = pack(rv[...], wide)
    for _, to, back in reversed(row_peers):
        @pl.when(to < row)
        def _():
            rows_to(to, back)

    loads[4].wait()
    loads[5].wait()
    half = order // 2
    uh, ul = split(du[...])
    lh, ll = split(dl[...])

    def product(rows, mid, cols):
        a, b = uh[rows, mid], ul[rows, mid]
        c, d = lh[mid, cols], ll[mid, cols]
        return dot(a, c) + (dot(a, d) + dot(b, c))

    lo, hi, full = slice(0, half), slice(half, order), slice(0, order)
    for rows, mid, cols in ((lo, full, lo), (lo, hi, hi), (hi, hi, lo), (hi, hi, hi)):
        mh[rows, cols], ml[rows, cols] = split(product(rows, mid, cols))

    @pl.when(higher_row > 0)
    def _():
        pl.semaphore_wait(row_hello, higher_row)
    for _, to, back in row_peers:
        @pl.when(to > row)
        def _():
            rows_to(to, back)

    @pl.when(higher_col > 0)
    def _():
        pl.semaphore_wait(col_hello, higher_col)
    for _, to, _ in near_cols:
        pl.when(to > col)(functools.partial(cols_to, to))

    def arrive(buf, slot, send, recv, step):
        row_copy(buf, slot, send, recv.at[step], mate).wait_recv()
        if paired:
            row_copy(buf, slot, send, recv.at[0], mate).start()

    for step, slot, _ in near:
        arrive(guall, slot, gu_send, gu_recv, step)
        arrive(gvall, slot, gv_send, gv_recv, step)

    def all_of(buf, count, send, recv):
        part = buf.at[pl.ds(0, count)]
        return pltpu.make_async_remote_copy(
            src_ref=part, dst_ref=part, send_sem=send, recv_sem=recv,
            device_id=(mate, col), device_id_type=MESH,
        )

    tiles = cvall.shape[1]
    loads[2].wait()
    loads[3].wait()
    loads[6].wait()
    if n_col > 1:
        all_of(cvall, n_col - 1, cv_send, cv_recv).wait_recv()
    weights = []
    for t in range(tiles):
        turned = jnp.concatenate([cvall[c, t] for c in range(n_col)], axis=-1)
        wh, wl = split(dot(turned, mh[...]) + dot(turned, ml[...]))
        weights.append(jnp.concatenate([wh, wl], axis=0))

    if n_col > 1:
        all_of(cuall, n_col - 1, cu_send, cu_recv).wait_recv()
    if paired:
        all_of(guall, chips, gu_send, gu_recv.at[0]).wait_recv()
    lanes = wide * rank
    spread = jnp.concatenate([guall[:, p].reshape(order, lanes) for p in range(pieces)], axis=-1)
    for t in range(tiles):
        turned = jnp.concatenate([cuall[c, t] for c in range(n_col)], axis=-1).astype(F32)
        left = jnp.concatenate([turned, turned], axis=0).T.astype(BF16)
        c = dot(weights[t], spread)
        ch, cl = split(c[:rank] + c[rank:])
        high, low = split(dot(left, jnp.concatenate([ch, cl], axis=0)))
        for p in range(pieces):
            at = slice(p * lanes, (p + 1) * lanes)
            d_ref[t * pieces + p] = jnp.concatenate([high[:, at], low[:, at]], axis=-1)

    if paired:
        all_of(gvall, chips, gv_send, gv_recv.at[0]).wait_recv()
    if n_col > 1:
        all_of(cvall, n_col - 1, cv_send, cv_recv).wait_send()
        all_of(cuall, n_col - 1, cu_send, cu_recv).wait_send()
    if n_row > 1:
        all_of(guall, n_row - 1, gu_send, gu_recv.at[0]).wait_send()
        all_of(gvall, n_row - 1, gv_send, gv_recv.at[0]).wait_send()


def update_kernel(blocks, rank, d_ref, gv_ref, trail, out_hbm, out, out_sem):
    n_row, pieces, rc, lanes = gv_ref.shape
    order = n_row * rc
    count = order // blocks
    wide = lanes // rank
    tiles = d_ref.shape[0] // pieces
    for p in range(pieces):
        part = gv_ref[:, p].reshape(order, lanes)
        tile_of = lax.broadcasted_iota(jnp.int32, part.shape, 1) // rank
        for w in range(wide):
            only = jnp.where(tile_of == w, part.astype(F32), 0.0).astype(BF16) if wide > 1 else part
            right = jnp.concatenate([only, only], axis=-1)
            for b in range(blocks):
                for t in range(tiles):
                    rows = pl.ds(t * order, order)
                    at = pl.ds((p * wide + w) * order + b * count, count)
                    product = dot_rt(d_ref[t * pieces + p], right[b * count:(b + 1) * count])
                    out[rows, at] = (trail[rows, at].astype(F32) - product).astype(BF16)
                    pltpu.make_async_copy(out.at[rows, at], out_hbm.at[rows, at], out_sem).start()
    pltpu.make_async_copy(out, out_hbm, out_sem).wait()


def shards(n_row, n_col, trailing, col_u, col_v, row_u, row_v, diag_lower_inv, diag_upper_inv):
    mt, cc, rank = col_u.shape
    nt, rc, _ = row_u.shape
    order = diag_lower_inv.shape[0]
    anywhere = pl.BlockSpec(memory_space=pl.ANY)
    dma = pltpu.SemaphoreType.DMA
    vmem = pl.BlockSpec(memory_space=pltpu.VMEM)
    wide = max(1, LANES // rank)
    wide = wide if nt % wide == 0 else 1
    chips = n_row // 2 if n_row % 2 == 0 else n_row
    panel = pltpu.VMEM((n_row, nt // wide, rc, wide * rank), BF16)
    handed = pl.pallas_call(
        functools.partial(panel_kernel, n_row, n_col, order, rank),
        out_shape=[
            pltpu.VMEM((mt * nt // wide, order, 2 * wide * rank), BF16),
            panel,
            pltpu.VMEM(trailing.shape, BF16),
        ],
        in_specs=[anywhere] * 7,
        out_specs=[vmem] * 3,
        scratch_shapes=[
            pltpu.VMEM(row_u.shape, BF16),
            pltpu.VMEM(row_v.shape, BF16),
            pltpu.VMEM((order, order), F32),
            pltpu.VMEM((order, order), F32),
            pltpu.VMEM((order, order), BF16),
            pltpu.VMEM((order, order), BF16),
            pltpu.VMEM((n_col, mt, rank, cc), BF16),
            pltpu.VMEM((n_col, mt, rank, cc), BF16),
            panel,
            dma((7,)), dma(()), dma(()), dma(()), dma(()),
            dma(()), dma((chips,)), dma(()), dma((chips,)),
            pltpu.SemaphoreType.REGULAR, pltpu.SemaphoreType.REGULAR,
        ],
        compiler_params=pltpu.CompilerParams(collective_id=0, has_side_effects=True),
        name="panels",
    )(
        jnp.swapaxes(col_u, 1, 2), jnp.swapaxes(col_v, 1, 2), row_u, row_v,
        diag_lower_inv, diag_upper_inv, trailing,
    )
    handed = [pltpu.with_memory_space_constraint(x, pltpu.VMEM) for x in handed]
    return pl.pallas_call(
        functools.partial(update_kernel, BLOCKS, rank),
        out_shape=jax.ShapeDtypeStruct(trailing.shape, BF16),
        in_specs=[vmem] * 3,
        out_specs=anywhere,
        scratch_shapes=[pltpu.VMEM(trailing.shape, BF16), dma(())],
        name="update",
    )(*handed)


def solution(mesh):
    placed = (
        P("row", "col"),
        P("row", "col", None),
        P("row", "col", None),
        P("col", "row", None),
        P("col", "row", None),
        P(),
        P(),
    )
    return jax.shard_map(
        functools.partial(shards, mesh.shape["row"], mesh.shape["col"]),
        mesh=mesh, in_specs=placed, out_specs=P("row", "col"), check_vma=False,
    )
```

time: 13.6 us -> 11 us (0.81)
  Pallas kernels: 13.4 us -> 10.8 us
    pallas_call x2, Pallas kernels: 13.4 us -> 10.8 us  [the longest x1 9.15 us: shards(): pl.pallas_call(functools.partial(panel_kernel, n_row, n_col, order, rank)...]
where the time goes in v2:
time: 11 us; the launch traced here: 10.8 us
  Pallas kernels  10.8 us (98%)
    pallas_call x1, Pallas kernels, shards(): pl.pallas_call(functools.partial(panel_kernel, n_row, n_col, order, rank)...  9.15 us
    pallas_call x1, Pallas kernels, shards(): pl.pallas_call(functools.partial(update_kernel, BLOCKS, rank), out_shape=...  1.66 us

profile of v2, /device:TPU:1, one launch (start us, length us, event | category | flops | bytes accessed | tf_op | source)
XLA Modules:
  0.0 10.8 jit_solution(11314798890056056574)
XLA Ops:
  0.0 9.2 %panels.1 = (bf16[2,512,256]{2,1,0:T(8,128)(2,1)S(1)}, bf16[8,2,64,128]{3,2,1,0:T(8,128)(2,1)S(1)}, bf16[512,2048]{1,0:T(8,128)(2,1)S(1)}) custom-call(bf16[1,64,128]{2,1,0:T(8,128)(2,1)} %bitcast.2, bf16[1,64,128]{2,1,0:T(8,128)(2,1)} %bitcast.3, bf16[4,64,64]{2,1,0:T(8,128)(2,1)} %ru_hbm.1, bf16[4,64,64]{2,1,0:T(8,128)(2,1)} %rv_hbm.1, f32[512,512]{1,0:T(8,128)} %dl_hbm.1, ...), custom_call_target="tpu_custom_call" | custom-call | tf_op jit(solution)/shard_map/panels/pallas_call | solution.py:263
  9.2 1.7 %update.1 = bf16[512,2048]{1,0:T(8,128)(2,1)} custom-call(bf16[2,512,256]{2,1,0:T(8,128)(2,1)S(1)} %get-tuple-element.8.d_ref, bf16[8,2,64,128]{3,2,1,0:T(8,128)(2,1)S(1)} %get-tuple-element.9.gv_ref, bf16[512,2048]{1,0:T(8,128)(2,1)S(1)} %get-tuple-element.10.trail), custom_call_target="tpu_custom_call" | custom-call | tf_op jit(solution)/shard_map/update/pallas_call | solution.py:293

commit v3 on v2

--- a/solution.py
+++ b/solution.py
@@ -55,7 +55,7 @@
     n_row, n_col, order, rank,
     cu_hbm, cv_hbm, ru_hbm, rv_hbm, dl_hbm, du_hbm, trail_hbm,
     d_ref, gvall, trail,
-    ru, rv, dl, du, mh, ml, cuall, cvall, guall,
+    own, diag, mh, ml, cuall, cvall, guall,
     in_sem, cu_send, cu_recv, cv_send, cv_recv, gu_send, gu_recv, gv_send, gv_recv,
     row_hello, col_hello,
 ):
@@ -67,13 +67,23 @@
     core = row % width
     chip = row // width
     mate = chip * width + (1 - core) if paired else row
-    nt, pieces = ru.shape[0], guall.shape[1]
+    nt, pieces = own.shape[1], guall.shape[1]
     wide = nt // pieces
 
     near = [(step, to * width + core, back) for step, to, back in others(chip, chips)]
     near_cols = others(col, n_col)
     row_peers = ([(0, mate, 0)] if paired else []) + near
 
+    def load(src, dst, sem):
+        copy = pltpu.make_async_copy(src, dst, sem)
+        copy.start()
+        return copy
+
+    load(ru_hbm, own.at[0], in_sem.at[0])
+    load(rv_hbm, own.at[1], in_sem.at[0])
+    load(cv_hbm, cvall.at[col], cv_recv)
+    load(cu_hbm, cuall.at[col], cu_recv)
+
     barrier = pltpu.get_barrier_semaphore()
     for _, to, _ in row_peers:
         @pl.when(to > row)
@@ -84,14 +94,9 @@
         def _():
             pl.semaphore_signal(barrier, inc=1, device_id=(row, to), device_id_type=MESH)
 
-    loads = []
-    for n, (src, dst) in enumerate([
-        (ru_hbm, ru), (rv_hbm, rv), (cv_hbm, cvall.at[col]), (cu_hbm, cuall.at[col]),
-        (dl_hbm, dl), (du_hbm, du), (trail_hbm, trail),
-    ]):
-        load = pltpu.make_async_copy(src, dst, in_sem.at[n])
-        load.start()
-        loads.append(load)
+    load(dl_hbm, diag.at[0], in_sem.at[1])
+    load(du_hbm, diag.at[1], in_sem.at[1])
+    trail_load = load(trail_hbm, trail, in_sem.at[2])
 
     lower_row = chip + (core if paired else 0)
     lower_col = col
@@ -101,15 +106,6 @@
     @pl.when(lower_row + lower_col > 0)
     def _():
         pl.semaphore_wait(barrier, lower_row + lower_col)
-
-    for _, to, _ in row_peers:
-        @pl.when(to < row)
-        def _():
-            pl.semaphore_signal(row_hello, inc=1, device_id=(to, col), device_id_type=MESH)
-    for _, to, _ in near_cols:
-        @pl.when(to < col)
-        def _():
-            pl.semaphore_signal(col_hello, inc=1, device_id=(row, to), device_id_type=MESH)
 
     def row_copy(buf, slot, send, recv, to):
         return pltpu.make_async_remote_copy(
@@ -135,29 +131,22 @@
         @pl.when(to < col)
         def _():
             cols_to(to)
-    loads[0].wait()
-    loads[1].wait()
-    guall[row] = pack(ru[...], wide)
-    gvall[row] = pack(rv[...], wide)
+    for _, to, _ in row_peers:
+        @pl.when(to < row)
+        def _():
+            pl.semaphore_signal(row_hello, inc=1, device_id=(to, col), device_id_type=MESH)
+    for _, to, _ in near_cols:
+        @pl.when(to < col)
+        def _():
+            pl.semaphore_signal(col_hello, inc=1, device_id=(row, to), device_id_type=MESH)
+
+    pltpu.make_async_copy(own, own, in_sem.at[0]).wait()
+    guall[row] = pack(own[0], wide)
+    gvall[row] = pack(own[1], wide)
     for _, to, back in reversed(row_peers):
         @pl.when(to < row)
         def _():
             rows_to(to, back)
-
-    loads[4].wait()
-    loads[5].wait()
-    half = order // 2
-    uh, ul = split(du[...])
-    lh, ll = split(dl[...])
-
-    def product(rows, mid, cols):
-        a, b = uh[rows, mid], ul[rows, mid]
-        c, d = lh[mid, cols], ll[mid, cols]
-        return dot(a, c) + (dot(a, d) + dot(b, c))
-
-    lo, hi, full = slice(0, half), slice(half, order), slice(0, order)
-    for rows, mid, cols in ((lo, full, lo), (lo, hi, hi), (hi, hi, lo), (hi, hi, hi)):
-        mh[rows, cols], ml[rows, cols] = split(product(rows, mid, cols))
 
     @pl.when(higher_row > 0)
     def _():
@@ -173,6 +162,20 @@
     for _, to, _ in near_cols:
         pl.when(to > col)(functools.partial(cols_to, to))
 
+    pltpu.make_async_copy(diag, diag, in_sem.at[1]).wait()
+    half = order // 2
+    uh, ul = split(diag[1])
+    lh, ll = split(diag[0])
+
+    def product(rows, mid, cols):
+        a, b = uh[rows, mid], ul[rows, mid]
+        c, d = lh[mid, cols], ll[mid, cols]
+        return dot(a, c) + (dot(a, d) + dot(b, c))
+
+    lo, hi, full = slice(0, half), slice(half, order), slice(0, order)
+    for rows, mid, cols in ((lo, full, lo), (lo, hi, hi), (hi, hi, lo), (hi, hi, hi)):
+        mh[rows, cols], ml[rows, cols] = split(product(rows, mid, cols))
+
     def arrive(buf, slot, send, recv, step):
         row_copy(buf, slot, send, recv.at[step], mate).wait_recv()
         if paired:
@@ -180,6 +183,7 @@
 
     for step, slot, _ in near:
         arrive(guall, slot, gu_send, gu_recv, step)
+    for step, slot, _ in near:
         arrive(gvall, slot, gv_send, gv_recv, step)
 
     def all_of(buf, count, send, recv):
@@ -190,19 +194,15 @@
         )
 
     tiles = cvall.shape[1]
-    loads[2].wait()
-    loads[3].wait()
-    loads[6].wait()
-    if n_col > 1:
-        all_of(cvall, n_col - 1, cv_send, cv_recv).wait_recv()
+    trail_load.wait()
+    all_of(cvall, n_col, cv_send, cv_recv).wait_recv()
     weights = []
     for t in range(tiles):
         turned = jnp.concatenate([cvall[c, t] for c in range(n_col)], axis=-1)
         wh, wl = split(dot(turned, mh[...]) + dot(turned, ml[...]))
         weights.append(jnp.concatenate([wh, wl], axis=0))
 
-    if n_col > 1:
-        all_of(cuall, n_col - 1, cu_send, cu_recv).wait_recv()
+    all_of(cuall, n_col, cu_send, cu_recv).wait_recv()
     if paired:
         all_of(guall, chips, gu_send, gu_recv.at[0]).wait_recv()
     lanes = wide * rank
@@ -270,16 +270,14 @@
         in_specs=[anywhere] * 7,
         out_specs=[vmem] * 3,
         scratch_shapes=[
-            pltpu.VMEM(row_u.shape, BF16),
-            pltpu.VMEM(row_v.shape, BF16),
-            pltpu.VMEM((order, order), F32),
-            pltpu.VMEM((order, order), F32),
+            pltpu.VMEM((2, *row_u.shape), BF16),
+            pltpu.VMEM((2, order, order), F32),
             pltpu.VMEM((order, order), BF16),
             pltpu.VMEM((order, order), BF16),
             pltpu.VMEM((n_col, mt, rank, cc), BF16),
             pltpu.VMEM((n_col, mt, rank, cc), BF16),
             panel,
-            dma((7,)), dma(()), dma(()), dma(()), dma(()),
+            dma((3,)), dma(()), dma(()), dma(()), dma(()),
             dma(()), dma((chips,)), dma(()), dma((chips,)),
             pltpu.SemaphoreType.REGULAR, pltpu.SemaphoreType.REGULAR,
         ],

time: 11 us -> 10.7 us (0.973)
  the two profiles are of different devices: /device:TPU:1 before, /device:TPU:28 now
where the time goes in v3:
time: 10.7 us; the launch traced here: 10.6 us
  Pallas kernels  10.6 us (99%)
    pallas_call x1, Pallas kernels, shards(): pl.pallas_call(functools.partial(panel_kernel, n_row, n_col, order, rank)...  8.93 us
    pallas_call x1, Pallas kernels, shards(): pl.pallas_call(functools.partial(update_kernel, BLOCKS, rank), out_shape=...  1.66 us

profile of v3, /device:TPU:28, one launch (start us, length us, event | category | flops | bytes accessed | tf_op | source)
XLA Modules:
  0.0 10.6 jit_solution(2635265432702969476)
XLA Ops:
  0.0 8.9 %panels.1 = (bf16[2,512,256]{2,1,0:T(8,128)(2,1)S(1)}, bf16[8,2,64,128]{3,2,1,0:T(8,128)(2,1)S(1)}, bf16[512,2048]{1,0:T(8,128)(2,1)S(1)}) custom-call(bf16[1,64,128]{2,1,0:T(8,128)(2,1)} %bitcast.2, bf16[1,64,128]{2,1,0:T(8,128)(2,1)} %bitcast.3, bf16[4,64,64]{2,1,0:T(8,128)(2,1)} %ru_hbm.1, bf16[4,64,64]{2,1,0:T(8,128)(2,1)} %rv_hbm.1, f32[512,512]{1,0:T(8,128)} %dl_hbm.1, ...), custom_call_target="tpu_custom_call" | custom-call | tf_op jit(solution)/shard_map/panels/pallas_call | solution.py:263
  8.9 1.7 %update.1 = bf16[512,2048]{1,0:T(8,128)(2,1)} custom-call(bf16[2,512,256]{2,1,0:T(8,128)(2,1)S(1)} %get-tuple-element.8.d_ref, bf16[8,2,64,128]{3,2,1,0:T(8,128)(2,1)S(1)} %get-tuple-element.9.gv_ref, bf16[512,2048]{1,0:T(8,128)(2,1)S(1)} %get-tuple-element.10.trail), custom_call_target="tpu_custom_call" | custom-call | tf_op jit(solution)/shard_map/update/pallas_call | solution.py:291

commit v4 on v3

--- a/solution.py
+++ b/solution.py
@@ -81,8 +81,8 @@
 
     load(ru_hbm, own.at[0], in_sem.at[0])
     load(rv_hbm, own.at[1], in_sem.at[0])
-    load(cv_hbm, cvall.at[col], cv_recv)
-    load(cu_hbm, cuall.at[col], cu_recv)
+    cv_load = load(cv_hbm, cvall.at[col], in_sem.at[3])
+    cu_load = load(cu_hbm, cuall.at[col], in_sem.at[4])
 
     barrier = pltpu.get_barrier_semaphore()
     for _, to, _ in row_peers:
@@ -119,9 +119,9 @@
             device_id=(row, to), device_id_type=MESH,
         )
 
-    def cols_to(to):
-        col_send(cv_hbm, cvall, cv_send, cv_recv, to).start()
-        col_send(cu_hbm, cuall, cu_send, cu_recv, to).start()
+    def cols_to(to, cv, cu):
+        col_send(cv, cvall, cv_send, cv_recv, to).start()
+        col_send(cu, cuall, cu_send, cu_recv, to).start()
 
     def rows_to(to, back):
         row_copy(guall, row, gu_send, gu_recv.at[back], to).start()
@@ -130,7 +130,7 @@
     for to in range(n_col):
         @pl.when(to < col)
         def _():
-            cols_to(to)
+            cols_to(to, cv_hbm, cu_hbm)
     for _, to, _ in row_peers:
         @pl.when(to < row)
         def _():
@@ -156,11 +156,14 @@
         def _():
             rows_to(to, back)
 
+    cv_load.wait()
+    cu_load.wait()
+
     @pl.when(higher_col > 0)
     def _():
         pl.semaphore_wait(col_hello, higher_col)
     for _, to, _ in near_cols:
-        pl.when(to > col)(functools.partial(cols_to, to))
+        pl.when(to > col)(functools.partial(cols_to, to, cvall.at[col], cuall.at[col]))
 
     pltpu.make_async_copy(diag, diag, in_sem.at[1]).wait()
     half = order // 2
@@ -195,14 +198,16 @@
 
     tiles = cvall.shape[1]
     trail_load.wait()
-    all_of(cvall, n_col, cv_send, cv_recv).wait_recv()
+    if n_col > 1:
+        all_of(cvall, n_col - 1, cv_send, cv_recv).wait_recv()
     weights = []
     for t in range(tiles):
         turned = jnp.concatenate([cvall[c, t] for c in range(n_col)], axis=-1)
         wh, wl = split(dot(turned, mh[...]) + dot(turned, ml[...]))
         weights.append(jnp.concatenate([wh, wl], axis=0))
 
-    all_of(cuall, n_col, cu_send, cu_recv).wait_recv()
+    if n_col > 1:
+        all_of(cuall, n_col - 1, cu_send, cu_recv).wait_recv()
     if paired:
         all_of(guall, chips, gu_send, gu_recv.at[0]).wait_recv()
     lanes = wide * rank
@@ -277,7 +282,7 @@
             pltpu.VMEM((n_col, mt, rank, cc), BF16),
             pltpu.VMEM((n_col, mt, rank, cc), BF16),
             panel,
-            dma((3,)), dma(()), dma(()), dma(()), dma(()),
+            dma((5,)), dma(()), dma(()), dma(()), dma(()),
             dma(()), dma((chips,)), dma(()), dma((chips,)),
             pltpu.SemaphoreType.REGULAR, pltpu.SemaphoreType.REGULAR,
         ],

time: 10.7 us -> 10.6 us (level)
  the two profiles are of different devices: /device:TPU:28 before, /device:TPU:0 now
where the time goes in v4:
time: 10.6 us; the launch traced here: 10.5 us
  Pallas kernels  10.5 us (99%)
    pallas_call x1, Pallas kernels, shards(): pl.pallas_call(functools.partial(panel_kernel, n_row, n_col, order, rank)...  8.83 us
    pallas_call x1, Pallas kernels, shards(): pl.pallas_call(functools.partial(update_kernel, BLOCKS, rank), out_shape=...  1.66 us

profile of v4, /device:TPU:0, one launch (start us, length us, event | category | flops | bytes accessed | tf_op | source)
XLA Modules:
  0.0 10.5 jit_solution(1167861566244831342)
XLA Ops:
  0.0 8.8 %panels.1 = (bf16[2,512,256]{2,1,0:T(8,128)(2,1)S(1)}, bf16[8,2,64,128]{3,2,1,0:T(8,128)(2,1)S(1)}, bf16[512,2048]{1,0:T(8,128)(2,1)S(1)}) custom-call(bf16[1,64,128]{2,1,0:T(8,128)(2,1)} %bitcast.2, bf16[1,64,128]{2,1,0:T(8,128)(2,1)} %bitcast.3, bf16[4,64,64]{2,1,0:T(8,128)(2,1)} %ru_hbm.1, bf16[4,64,64]{2,1,0:T(8,128)(2,1)} %rv_hbm.1, f32[512,512]{1,0:T(8,128)} %dl_hbm.1, ...), custom_call_target="tpu_custom_call" | custom-call | tf_op jit(solution)/shard_map/panels/pallas_call | solution.py:268
  8.8 1.7 %update.1 = bf16[512,2048]{1,0:T(8,128)(2,1)} custom-call(bf16[2,512,256]{2,1,0:T(8,128)(2,1)S(1)} %get-tuple-element.8.d_ref, bf16[8,2,64,128]{3,2,1,0:T(8,128)(2,1)S(1)} %get-tuple-element.9.gv_ref, bf16[512,2048]{1,0:T(8,128)(2,1)S(1)} %get-tuple-element.10.trail), custom_call_target="tpu_custom_call" | custom-call | tf_op jit(solution)/shard_map/update/pallas_call | solution.py:296

commit v5 on v4

--- a/solution.py
+++ b/solution.py
@@ -100,8 +100,6 @@
 
     lower_row = chip + (core if paired else 0)
     lower_col = col
-    higher_row = len(row_peers) - lower_row
-    higher_col = len(near_cols) - lower_col
 
     @pl.when(lower_row + lower_col > 0)
     def _():
@@ -131,14 +129,14 @@
         @pl.when(to < col)
         def _():
             cols_to(to, cv_hbm, cu_hbm)
-    for _, to, _ in row_peers:
+    for _, to, back in row_peers:
         @pl.when(to < row)
         def _():
-            pl.semaphore_signal(row_hello, inc=1, device_id=(to, col), device_id_type=MESH)
-    for _, to, _ in near_cols:
+            pl.semaphore_signal(row_hello.at[back], inc=1, device_id=(to, col), device_id_type=MESH)
+    for _, to, back in near_cols:
         @pl.when(to < col)
         def _():
-            pl.semaphore_signal(col_hello, inc=1, device_id=(row, to), device_id_type=MESH)
+            pl.semaphore_signal(col_hello.at[back], inc=1, device_id=(row, to), device_id_type=MESH)
 
     pltpu.make_async_copy(own, own, in_sem.at[0]).wait()
     guall[row] = pack(own[0], wide)
@@ -148,22 +146,33 @@
         def _():
             rows_to(to, back)
 
-    @pl.when(higher_row > 0)
-    def _():
-        pl.semaphore_wait(row_hello, higher_row)
-    for _, to, back in row_peers:
-        @pl.when(to > row)
-        def _():
-            rows_to(to, back)
-
     cv_load.wait()
     cu_load.wait()
 
-    @pl.when(higher_col > 0)
-    def _():
-        pl.semaphore_wait(col_hello, higher_col)
-    for _, to, _ in near_cols:
-        pl.when(to > col)(functools.partial(cols_to, to, cvall.at[col], cuall.at[col]))
+    def greeted_row(step, to, back):
+        @pl.when(to > row)
+        def _():
+            pl.semaphore_wait(row_hello.at[step], 1)
+            rows_to(to, back)
+
+    def greeted_col(step, to):
+        @pl.when(to > col)
+        def _():
+            pl.semaphore_wait(col_hello.at[step], 1)
+            cols_to(to, cvall.at[col], cuall.at[col])
+
+    if paired:
+        greeted_row(0, mate, 0)
+    for n in range(max(len(near), len(near_cols))):
+        if n == 0 and len(near) > 1:
+            greeted_row(*near[0])
+            greeted_row(*near[1])
+        elif n > 0 and n + 1 < len(near):
+            greeted_row(*near[n + 1])
+        elif n == 0 and near:
+            greeted_row(*near[0])
+        if n < len(near_cols):
+            greeted_col(*near_cols[n][:2])
 
     pltpu.make_async_copy(diag, diag, in_sem.at[1]).wait()
     half = order // 2
@@ -217,10 +226,10 @@
         left = jnp.concatenate([turned, turned], axis=0).T.astype(BF16)
         c = dot(weights[t], spread)
         ch, cl = split(c[:rank] + c[rank:])
-        high, low = split(dot(left, jnp.concatenate([ch, cl], axis=0)))
+        high = dot(left, jnp.concatenate([ch, cl], axis=0)).astype(BF16)
         for p in range(pieces):
             at = slice(p * lanes, (p + 1) * lanes)
-            d_ref[t * pieces + p] = jnp.concatenate([high[:, at], low[:, at]], axis=-1)
+            d_ref[t * pieces + p] = high[:, at]
 
     if paired:
         all_of(gvall, chips, gv_send, gv_recv.at[0]).wait_recv()
@@ -243,7 +252,7 @@
         tile_of = lax.broadcasted_iota(jnp.int32, part.shape, 1) // rank
         for w in range(wide):
             only = jnp.where(tile_of == w, part.astype(F32), 0.0).astype(BF16) if wide > 1 else part
-            right = jnp.concatenate([only, only], axis=-1)
+            right = only
             for b in range(blocks):
                 for t in range(tiles):
                     rows = pl.ds(t * order, order)
@@ -268,7 +277,7 @@
     handed = pl.pallas_call(
         functools.partial(panel_kernel, n_row, n_col, order, rank),
         out_shape=[
-            pltpu.VMEM((mt * nt // wide, order, 2 * wide * rank), BF16),
+            pltpu.VMEM((mt * nt // wide, order, wide * rank), BF16),
             panel,
             pltpu.VMEM(trailing.shape, BF16),
         ],
@@ -284,7 +293,7 @@
             panel,
             dma((5,)), dma(()), dma(()), dma(()), dma(()),
             dma(()), dma((chips,)), dma(()), dma((chips,)),
-            pltpu.SemaphoreType.REGULAR, pltpu.SemaphoreType.REGULAR,
+            pltpu.SemaphoreType.REGULAR((chips,)), pltpu.SemaphoreType.REGULAR((n_col,)),
         ],
         compiler_params=pltpu.CompilerParams(collective_id=0, has_side_effects=True),
         name="panels",

time: 10.6 us -> 10.7 us (level)
  no operation moved by 1% of the time
where the time goes in v5:
time: 10.7 us; the launch traced here: 10.5 us
  Pallas kernels  10.5 us (98%)
    pallas_call x1, Pallas kernels, shards(): pl.pallas_call(functools.partial(panel_kernel, n_row, n_col, order, rank)...  8.88 us
    pallas_call x1, Pallas kernels, shards(): pl.pallas_call(functools.partial(update_kernel, BLOCKS, rank), out_shape=...  1.62 us

profile of v5, /device:TPU:0, one launch (start us, length us, event | category | flops | bytes accessed | tf_op | source)
XLA Modules:
  0.0 10.5 jit_solution(12135570667537486020)
XLA Ops:
  0.0 8.9 %panels.1 = (bf16[2,512,128]{2,1,0:T(8,128)(2,1)S(1)}, bf16[8,2,64,128]{3,2,1,0:T(8,128)(2,1)S(1)}, bf16[512,2048]{1,0:T(8,128)(2,1)S(1)}) custom-call(bf16[1,64,128]{2,1,0:T(8,128)(2,1)} %bitcast.2, bf16[1,64,128]{2,1,0:T(8,128)(2,1)} %bitcast.3, bf16[4,64,64]{2,1,0:T(8,128)(2,1)} %ru_hbm.1, bf16[4,64,64]{2,1,0:T(8,128)(2,1)} %rv_hbm.1, f32[512,512]{1,0:T(8,128)} %dl_hbm.1, ...), custom_call_target="tpu_custom_call" | custom-call | tf_op jit(solution)/shard_map/panels/pallas_call | solution.py:277
  8.9 1.6 %update.1 = bf16[512,2048]{1,0:T(8,128)(2,1)} custom-call(bf16[2,512,128]{2,1,0:T(8,128)(2,1)S(1)} %get-tuple-element.8.d_ref, bf16[8,2,64,128]{3,2,1,0:T(8,128)(2,1)S(1)} %get-tuple-element.9.gv_ref, bf16[512,2048]{1,0:T(8,128)(2,1)S(1)} %get-tuple-element.10.trail), custom_call_target="tpu_custom_call" | custom-call | tf_op jit(solution)/shard_map/update/pallas_call | solution.py:305

commit v6 on v5

--- a/solution.py
+++ b/solution.py
@@ -129,15 +129,6 @@
         @pl.when(to < col)
         def _():
             cols_to(to, cv_hbm, cu_hbm)
-    for _, to, back in row_peers:
-        @pl.when(to < row)
-        def _():
-            pl.semaphore_signal(row_hello.at[back], inc=1, device_id=(to, col), device_id_type=MESH)
-    for _, to, back in near_cols:
-        @pl.when(to < col)
-        def _():
-            pl.semaphore_signal(col_hello.at[back], inc=1, device_id=(row, to), device_id_type=MESH)
-
     pltpu.make_async_copy(own, own, in_sem.at[0]).wait()
     guall[row] = pack(own[0], wide)
     gvall[row] = pack(own[1], wide)
@@ -145,6 +136,15 @@
         @pl.when(to < row)
         def _():
             rows_to(to, back)
+
+    for _, to, back in row_peers:
+        @pl.when(to < row)
+        def _():
+            pl.semaphore_signal(row_hello.at[back], inc=1, device_id=(to, col), device_id_type=MESH)
+    for _, to, back in near_cols:
+        @pl.when(to < col)
+        def _():
+            pl.semaphore_signal(col_hello.at[back], inc=1, device_id=(row, to), device_id_type=MESH)
 
     cv_load.wait()
     cu_load.wait()

time: 10.7 us -> 10.7 us (level)
  no operation moved by 1% of the time
where the time goes in v6:
time: 10.7 us; the launch traced here: 10.5 us
  Pallas kernels  10.5 us (98%)
    pallas_call x1, Pallas kernels, shards(): pl.pallas_call(functools.partial(panel_kernel, n_row, n_col, order, rank)...  8.88 us
    pallas_call x1, Pallas kernels, shards(): pl.pallas_call(functools.partial(update_kernel, BLOCKS, rank), out_shape=...  1.62 us

profile of v6, /device:TPU:0, one launch (start us, length us, event | category | flops | bytes accessed | tf_op | source)
XLA Modules:
  0.0 10.5 jit_solution(14170003661010207180)
XLA Ops:
  0.0 8.9 %panels.1 = (bf16[2,512,128]{2,1,0:T(8,128)(2,1)S(1)}, bf16[8,2,64,128]{3,2,1,0:T(8,128)(2,1)S(1)}, bf16[512,2048]{1,0:T(8,128)(2,1)S(1)}) custom-call(bf16[1,64,128]{2,1,0:T(8,128)(2,1)} %bitcast.2, bf16[1,64,128]{2,1,0:T(8,128)(2,1)} %bitcast.3, bf16[4,64,64]{2,1,0:T(8,128)(2,1)} %ru_hbm.1, bf16[4,64,64]{2,1,0:T(8,128)(2,1)} %rv_hbm.1, f32[512,512]{1,0:T(8,128)} %dl_hbm.1, ...), custom_call_target="tpu_custom_call" | custom-call | tf_op jit(solution)/shard_map/panels/pallas_call | solution.py:277
  8.9 1.6 %update.1 = bf16[512,2048]{1,0:T(8,128)(2,1)} custom-call(bf16[2,512,128]{2,1,0:T(8,128)(2,1)S(1)} %get-tuple-element.8.d_ref, bf16[8,2,64,128]{3,2,1,0:T(8,128)(2,1)S(1)} %get-tuple-element.9.gv_ref, bf16[512,2048]{1,0:T(8,128)(2,1)S(1)} %get-tuple-element.10.trail), custom_call_target="tpu_custom_call" | custom-call | tf_op jit(solution)/shard_map/update/pallas_call | solution.py:305

commit v7 on v6

--- a/solution.py
+++ b/solution.py
@@ -141,10 +141,10 @@
         @pl.when(to < row)
         def _():
             pl.semaphore_signal(row_hello.at[back], inc=1, device_id=(to, col), device_id_type=MESH)
-    for _, to, back in near_cols:
+    for _, to, _ in near_cols:
         @pl.when(to < col)
         def _():
-            pl.semaphore_signal(col_hello.at[back], inc=1, device_id=(row, to), device_id_type=MESH)
+            pl.semaphore_signal(col_hello, inc=1, device_id=(row, to), device_id_type=MESH)
 
     cv_load.wait()
     cu_load.wait()
@@ -155,15 +155,9 @@
             pl.semaphore_wait(row_hello.at[step], 1)
             rows_to(to, back)
 
-    def greeted_col(step, to):
-        @pl.when(to > col)
-        def _():
-            pl.semaphore_wait(col_hello.at[step], 1)
-            cols_to(to, cvall.at[col], cuall.at[col])
-
     if paired:
         greeted_row(0, mate, 0)
-    for n in range(max(len(near), len(near_cols))):
+    for n in range(len(near)):
         if n == 0 and len(near) > 1:
             greeted_row(*near[0])
             greeted_row(*near[1])
@@ -171,8 +165,14 @@
             greeted_row(*near[n + 1])
         elif n == 0 and near:
             greeted_row(*near[0])
-        if n < len(near_cols):
-            greeted_col(*near_cols[n][:2])
+
+    higher_col = len(near_cols) - col
+
+    @pl.when(higher_col > 0)
+    def _():
+        pl.semaphore_wait(col_hello, higher_col)
+    for _, to, _ in near_cols:
+        pl.when(to > col)(functools.partial(cols_to, to, cvall.at[col], cuall.at[col]))
 
     pltpu.make_async_copy(diag, diag, in_sem.at[1]).wait()
     half = order // 2
@@ -293,7 +293,7 @@
             panel,
             dma((5,)), dma(()), dma(()), dma(()), dma(()),
             dma(()), dma((chips,)), dma(()), dma((chips,)),
-            pltpu.SemaphoreType.REGULAR((chips,)), pltpu.SemaphoreType.REGULAR((n_col,)),
+            pltpu.SemaphoreType.REGULAR((chips,)), pltpu.SemaphoreType.REGULAR,
         ],
         compiler_params=pltpu.CompilerParams(collective_id=0, has_side_effects=True),
         name="panels",

time: 10.7 us -> 10.7 us (level)
  the two profiles are of different devices: /device:TPU:0 before, /device:TPU:28 now
where the time goes in v7:
time: 10.7 us; the launch traced here: 10.6 us
  Pallas kernels  10.6 us (99%)
    pallas_call x1, Pallas kernels, shards(): pl.pallas_call(functools.partial(panel_kernel, n_row, n_col, order, rank)...  8.95 us
    pallas_call x1, Pallas kernels, shards(): pl.pallas_call(functools.partial(update_kernel, BLOCKS, rank), out_shape=...  1.62 us

profile of v7, /device:TPU:28, one launch (start us, length us, event | category | flops | bytes accessed | tf_op | source)
XLA Modules:
  0.0 10.6 jit_solution(13092484914425819451)
XLA Ops:
  0.0 9.0 %panels.1 = (bf16[2,512,128]{2,1,0:T(8,128)(2,1)S(1)}, bf16[8,2,64,128]{3,2,1,0:T(8,128)(2,1)S(1)}, bf16[512,2048]{1,0:T(8,128)(2,1)S(1)}) custom-call(bf16[1,64,128]{2,1,0:T(8,128)(2,1)} %bitcast.2, bf16[1,64,128]{2,1,0:T(8,128)(2,1)} %bitcast.3, bf16[4,64,64]{2,1,0:T(8,128)(2,1)} %ru_hbm.1, bf16[4,64,64]{2,1,0:T(8,128)(2,1)} %rv_hbm.1, f32[512,512]{1,0:T(8,128)} %dl_hbm.1, ...), custom_call_target="tpu_custom_call" | custom-call | tf_op jit(solution)/shard_map/panels/pallas_call | solution.py:277
  9.0 1.6 %update.1 = bf16[512,2048]{1,0:T(8,128)(2,1)} custom-call(bf16[2,512,128]{2,1,0:T(8,128)(2,1)S(1)} %get-tuple-element.8.d_ref, bf16[8,2,64,128]{3,2,1,0:T(8,128)(2,1)S(1)} %get-tuple-element.9.gv_ref, bf16[512,2048]{1,0:T(8,128)(2,1)S(1)} %get-tuple-element.10.trail), custom_call_target="tpu_custom_call" | custom-call | tf_op jit(solution)/shard_map/update/pallas_call | solution.py:305
